TPU v7x, 32 devices: a whole 2x2x4 slice. The times are simulated.
32 devices in a mesh: dp: 8 (over z, y), mp: 4 (over x, core).
Axes of the slice: x: 2, y: 2, z: 4, core: 2. Of those that a mesh axis runs over, the one named last changes fastest.
Arguments:
- queries: bfloat16 [1024, 8192], P('dp', 'mp'), may hold values from -8 to 8
- tree_keys: bfloat16 [1024, 1024], P('dp', 'mp'), may hold values from -18 to 18
- tree_values: bfloat16 [1024, 1024], P('dp', 'mp'), may hold values from -6 to 6
- cache_keys: bfloat16 [16, 4096, 1024], P('dp', None, 'mp'), may hold values from -8 to 8
- cache_values: bfloat16 [16, 4096, 1024], P('dp', None, 'mp'), may hold values from -6 to 6
- cache_lens: int32 [16], P('dp'), may hold values from 1024 to 4096, as said below
- parents: int32 [16, 64], P('dp'), may hold values from -1 to 62, as said below
- accepted_nodes: int32 [16, 8], P('dp'), may hold values from 0 to 63, as said below
- residual: bfloat16 [1024, 8192], P('dp', 'mp'), may hold values from -1.796875 to 1.796875
- out_weight: bfloat16 [8192, 8192], P('mp', 'dp'), may hold values from -0.0625 to 0.0625
Outputs:
- tree_hidden: bfloat16 [1024, 8192], P('dp', 'mp')
- accepted_hidden: bfloat16 [128, 8192], P(None, 'mp')
Inputs may be any that keep to these rules, and one draw needn't show every extreme that they name: parents[r, 0] = -1 and 0 <= parents[r, i] < i for i >= 1. accepted_nodes[r, 0] = 0, the nodes of a row increase, and parents[r, accepted_nodes[r, a + 1]] = accepted_nodes[r, a]. `cache_lens`: some request has exactly 4096 filled positions.
All inputs are finite; a program needn't handle non-finite values.
Results may differ from a plain program's by a relative error of at most 0.015.
Values may be sent and summed in bfloat16 or wider, within the bound.
A program may use at most 64 MiB of HBM per device.

v0:
```python
import math
import jax
import jax.numpy as jnp
from jax import lax
from jax.sharding import PartitionSpec as P

HEADS = 64
KV_HEADS = 8
HD = 128
neg_large = -1e30


def ancestry(parents, node_count):
    positions = jnp.arange(node_count, dtype=jnp.int32)
    parent_hot = (parents[:, :, None] == positions[None, None, :]).astype(jnp.float32)
    reached = parent_hot + jnp.eye(node_count, dtype=jnp.float32)[None]
    for squaring in range((node_count - 1).bit_length()):
        reached = jnp.minimum(
            jnp.einsum("rij,rjk->rik", reached, reached, precision=lax.Precision.HIGHEST), 1.0
        )
    return reached > 0.5


def per_device(
    queries,
    tree_keys,
    tree_values,
    cache_keys,
    cache_values,
    cache_lens,
    parents,
    accepted_nodes,
    residual,
    out_weight,
):
    request_count = parents.shape[0]
    node_count = parents.shape[1]
    cache_length = cache_keys.shape[1]
    kv_local = tree_keys.shape[1] // HD
    group_size = HEADS // KV_HEADS
    scale_factor = 1.0 / math.sqrt(HD)
    query_grid = queries.reshape(request_count, node_count, kv_local, group_size, HD)
    tree_key_grid = tree_keys.reshape(request_count, node_count, kv_local, HD)
    tree_value_grid = tree_values.reshape(request_count, node_count, kv_local, HD)
    cache_key_grid = cache_keys.reshape(request_count, cache_length, kv_local, HD)
    cache_value_grid = cache_values.reshape(request_count, cache_length, kv_local, HD)
    ancestor = ancestry(parents, node_count)
    tree_scores = (
        jnp.einsum(
            "rnkgd,rjkd->rnkgj", query_grid, tree_key_grid, preferred_element_type=jnp.float32
        )
        * scale_factor
    )
    tree_scores = jnp.where(ancestor[:, :, None, None, :], tree_scores, neg_large)
    run_max = jnp.max(tree_scores, axis=-1)
    tree_weights = jnp.exp(tree_scores - run_max[..., None])
    run_sum = jnp.sum(tree_weights, axis=-1)
    run_acc = jnp.einsum(
        "rnkgj,rjkd->rnkgd",
        tree_weights.astype(jnp.bfloat16),
        tree_value_grid,
        preferred_element_type=jnp.float32,
    )
    block_len = min(512, cache_length)

    def absorb(block_number, state_now):
        old_max, old_sum, old_acc = state_now
        block_start = block_number * block_len
        key_block = lax.dynamic_slice_in_dim(cache_key_grid, block_start, block_len, 1)
        value_block = lax.dynamic_slice_in_dim(cache_value_grid, block_start, block_len, 1)
        block_scores = (
            jnp.einsum(
                "rnkgd,rpkd->rnkgp", query_grid, key_block, preferred_element_type=jnp.float32
            )
            * scale_factor
        )
        positions = block_start + jnp.arange(block_len, dtype=jnp.int32)
        live_keys = positions[None, :] < cache_lens[:, None]
        block_scores = jnp.where(live_keys[:, None, None, None, :], block_scores, neg_large)
        new_max = jnp.maximum(old_max, jnp.max(block_scores, axis=-1))
        block_weights = jnp.exp(block_scores - new_max[..., None])
        rescale = jnp.exp(old_max - new_max)
        new_sum = old_sum * rescale + jnp.sum(block_weights, axis=-1)
        new_acc = old_acc * rescale[..., None] + jnp.einsum(
            "rnkgp,rpkd->rnkgd",
            block_weights.astype(jnp.bfloat16),
            value_block,
            preferred_element_type=jnp.float32,
        )
        return (new_max, new_sum, new_acc)

    trip_count = cache_length // block_len
    run_max, run_sum, run_acc = lax.fori_loop(0, trip_count, absorb, (run_max, run_sum, run_acc))
    attended = (run_acc / run_sum[..., None]).astype(jnp.bfloat16)
    attended = attended.reshape(request_count * node_count, kv_local * group_size * HD)
    feature_share = residual.shape[1]
    all_rows = jnp.dot(
        lax.all_gather(attended, "dp", axis=0, tiled=True),
        out_weight,
        preferred_element_type=jnp.float32,
    )
    partial_sum = lax.all_to_all(
        all_rows.astype(jnp.bfloat16), "dp", split_axis=0, concat_axis=1, tiled=True
    ).astype(all_rows.dtype)
    head_total_sum = lax.psum(partial_sum.astype(jnp.bfloat16), "mp").astype(jnp.float32)
    own_share = lax.dynamic_slice_in_dim(
        head_total_sum, lax.axis_index("mp") * feature_share, feature_share, 1
    )
    tree_hidden = (residual.astype(jnp.float32) + own_share).astype(jnp.bfloat16)
    row_base = jnp.arange(request_count, dtype=jnp.int32)[:, None] * node_count
    picked_rows = (row_base + accepted_nodes).reshape(-1)
    picked_hidden = jnp.take(tree_hidden, picked_rows, axis=0)
    accepted_hidden = lax.all_gather(picked_hidden, "dp", axis=0, tiled=True)
    return (tree_hidden, accepted_hidden)


def solution(mesh):
    placed = (
        P("dp", "mp"),
        P("dp", "mp"),
        P("dp", "mp"),
        P("dp", None, "mp"),
        P("dp", None, "mp"),
        P("dp"),
        P("dp", None),
        P("dp", None),
        P("dp", "mp"),
        P("mp", "dp"),
    )
    return jax.shard_map(
        per_device,
        mesh=mesh,
        in_specs=placed,
        out_specs=(P("dp", "mp"), P(None, "mp")),
        check_vma=False,
    )
```

profile of v0, /device:TPU:0, one launch (start us, length us, event | category | flops | bytes accessed | tf_op | source)
XLA Modules:
  0.0 305.0 jit_solution(8466349382810361783)
XLA Ops:
  13.3 6.4 %copy.23 = bf16[2,4096,256]{1,2,0:T(8,128)(2,1)} copy(bf16[2,4096,256]{2,1,0:T(8,128)(2,1)} %param.15) | data formatting | bytes 8388608 | tf_op args[3]
  19.7 6.4 %copy.24 = bf16[2,4096,256]{1,2,0:T(8,128)(2,1)} copy(bf16[2,4096,256]{2,1,0:T(8,128)(2,1)} %param.16) | data formatting | bytes 8388608 | tf_op args[4]
  26.1 49.3 %while.17 = (s32[]{:T(128)}, f32[2,64,2,8]{1,3,2,0:T(8,128)S(1)}, f32[2,64,2,8]{1,3,2,0:T(8,128)S(1)}, f32[2,64,2,8,128]{4,1,3,2,0:T(8,128)S(1)}, s32[2]{0:T(128...) while((s32[]{:T(128)}, f32[2,64,2,8]{1,3,2,0:T(8,128)S(1)}, ...), condition=%wide.region_5.6_spmd, body=%wide.region_2.5_spmd.sunk | while | flops 548935168 | bytes 16392375 | solution.py:93
  26.2 1.8 bitcast_reduce_fusion.2
  28.0 1.7 fusion.61
  29.7 2.5 fusion.62
  32.3 1.8 bitcast_reduce_fusion.2
  34.2 1.7 fusion.61
  35.9 2.5 fusion.62
  38.5 1.8 bitcast_reduce_fusion.2
  40.3 1.7 fusion.61
  42.1 2.5 fusion.62
  44.7 1.8 bitcast_reduce_fusion.2
  46.5 1.7 fusion.61
  48.2 2.5 fusion.62
  50.8 1.8 bitcast_reduce_fusion.2
  52.7 1.7 fusion.61
  54.4 2.5 fusion.62
  57.0 1.8 bitcast_reduce_fusion.2
  58.9 1.7 fusion.61
  60.6 2.5 fusion.62
  63.2 1.8 bitcast_reduce_fusion.2
  65.0 1.7 fusion.61
  66.7 2.5 fusion.62
  69.3 1.8 bitcast_reduce_fusion.2
  71.2 1.7 fusion.61
  72.9 2.5 fusion.62
  77.2 75.6 %all-gather.2.cloned.1.call-done = bf16[1024,2048]{1,0:T(8,128)(2,1)} async-done(((bf16[128,2048]{1,0:T(8,128)(2,1)}), bf16[1024,2048]{1,0:T(8,128)(2,1)}) %all-gather.2.cloned.1.call-update) | async-done | bytes 4194320 | tf_op jit(solution)/shard_map/all_gather | solution.py:98
  152.8 7.9 %convolution_convert_fusion = bf16[1024,1024]{1,0:T(8,128)(2,1)S(1)} fusion(bf16[1024,2048]{1,0:T(8,128)(2,1)} %all-gather.2.cloned.1.call-done, bf16[2048,1024]{1,0:T(8,128)(2,1)} %param.21), kind=kOutput, calls=%fused_computation.27 | convolution fusion | flops 4296015872 | bytes 10485760 | tf_op jit(solution)/shard_map/dot_general | solution.py:97
  160.8 51.1 %all_to_all.19 = bf16[8,128,1024]{2,1,0:T(8,128)(2,1)S(1)} all-to-all(bf16[8,128,1024]{2,1,0:T(8,128)(2,1)S(1)} %bitcast.87), channel_id=1, replica_groups=mesh['dp'=8,'mp'=4] {'dp'}, dimensions={0} | all-to-all | bytes 4194304 | tf_op jit(solution)/shard_map/all_to_all | solution.py:102
  213.7 50.2 %all-reduce.2.cloned.1.call-done = bf16[128,8192]{1,0:T(8,128)(2,1)} async-done(((bf16[128,8192]{1,0:T(8,128)(2,1)}), bf16[128,8192]{1,0:T(8,128)(2,1)}) %all-reduce.2.cloned.1.call-update) | async-done | bytes 2097168 | tf_op jit(solution)/shard_map/psum | solution.py:105
  265.7 31.6 %all_gather.7 = bf16[128,2048]{1,0:T(8,128)(2,1)S(1)} all-gather(bf16[16,2048]{1,0:T(8,128)(2,1)S(1)} %broadcast_select_fusion), channel_id=1, replica_groups=mesh['dp'=8,'mp'=4] {'dp'}, dimensions={0}, use_global_device_ids=true | all-gather | bytes 589824 | tf_op jit(solution)/shard_map/all_gather | solution.py:113
  (86 shorter events, 13.0 us)
Async XLA Ops:
  7.2 5.6 %copy-start.2 = (bf16[128,256]{1,0:T(8,128)(2,1)S(1)}, bf16[128,256]{1,0:T(8,128)(2,1)}, u32[]{:S(2)}) copy-start(bf16[128,256]{1,0:T(8,128)(2,1)} %param.14) | copy-start | bytes 196612
  7.2 145.7 %all-gather.2.cloned.1.call-start = ((), (), s32[]{:S(2)}) async-start(), calls=%async_computation.1 | async-start | bytes 4718592 | tf_op jit(solution)/shard_map/all_gather | solution.py:98
  19.7 6.4 %copy-start.3 = (s32[2]{0:T(128)S(1)}, s32[2]{0:T(128)}, u32[]{:S(2)}) copy-start(s32[2]{0:T(128)} %param.17) | copy-start | bytes 28
  77.2 186.7 %all-reduce.2.cloned.1.call-start = ((), (), s32[]{:S(2)}) async-start(), calls=%async_computation.2 | async-start | bytes 4194304 | tf_op jit(solution)/shard_map/psum | solution.py:105
  211.9 1.5 copy-start.4
  211.9 51.9 %copy-start.1 = (bf16[128,2048]{1,0:T(8,128)(2,1)S(1)}, bf16[128,2048]{1,0:T(8,128)(2,1)}, u32[]{:S(2)}) copy-start(bf16[128,2048]{1,0:T(8,128)(2,1)} %param.20) | copy-start | bytes 1572868
  265.1 33.1 %copy-start = (bf16[128,2048]{1,0:T(8,128)(2,1)}, bf16[128,2048]{1,0:T(8,128)(2,1)S(1)}, u32[]{:S(2)}) copy-start(bf16[128,2048]{1,0:T(8,128)(2,1)S(1)} %add_convert_fusion) | copy-start | bytes 1572868
Sparse Core Ops, SparseCore 0:
  77.3 75.5 all-gather.1
  213.5 50.2 all-reduce.1
where the time goes:
time: 306 us; the launch traced here: 305 us
  waiting for transfers between devices  126 us (41%)
  blocking collectives  82.7 us (27%)
  matrix products  45.3 us (15%)
  local copies, waits for them, and re-layouts  20 us (7%)
  other arithmetic  16.3 us (5%)
  between operations  14.2 us (5%)
    all_gather x1, waiting for transfers between devices, per_device(): lax.all_gather(attended, 'dp', axis=0, tiled=True)  75.6 us
    all_to_all x1, blocking collectives, per_device(): lax.all_to_all(all_rows.astype(jnp.bfloat16), 'dp', split_axis=0, concat_...  51.1 us
    psum x1, waiting for transfers between devices, per_device(): lax.psum(partial_sum.astype(jnp.bfloat16), 'mp').astype(jnp.float32)  50.2 us
    all_gather x1, blocking collectives, per_device(): accepted_hidden = lax.all_gather(picked_hidden, 'dp', axis=0, tiled=True)  31.6 us
    dot_general x8, matrix products, absorb(): jnp.einsum('rnkgp,rpkd->rnkgd', block_weights.astype(jnp.bfloat16), value...  19.8 us
    unnamed x14, local copies, waits for them, and re-layouts  14.7 us
    dot_general x8, matrix products, absorb(): jnp.einsum('rnkgd,rpkd->rnkgp', query_grid, key_block, preferred_element_...  14.7 us
    reduce_sum x8, other arithmetic, absorb(): new_sum = old_sum * rescale + jnp.sum(block_weights, axis=-1)  13.6 us
  transfers between devices with their start and end apart: 2, of which 2 were waited for; matrix products, arithmetic and copies ran while one was open for 0% of the time, Pallas kernels for 0%

commit v1 on v0

--- a/solution.py
+++ b/solution.py
@@ -1,3 +1,4 @@
+import functools
 import math
 import jax
 import jax.numpy as jnp
@@ -8,6 +9,24 @@
 KV_HEADS = 8
 HD = 128
 neg_large = -1e30
+
+
+def turn_map_over_axis(frame, device_axis, out_dim):
+    nodes = lax.axis_size(device_axis)
+    all_blocks = [frame]
+    for idx in range(nodes - 1):
+        all_blocks.append(
+            lax.ppermute(all_blocks[-1], device_axis, [(d, (d + 1) % nodes) for d in range(nodes)])
+        )
+    left_arr = jnp.roll(
+        jnp.concatenate(all_blocks[::-1], out_dim),
+        (lax.axis_index(device_axis) + 1) * frame.shape[out_dim],
+        out_dim,
+    )
+    return left_arr
+
+
+open_surface_on_mesh = functools.partial(turn_map_over_axis, device_axis="dp", out_dim=0)
 
 
 def ancestry(parents, node_count):
@@ -110,7 +129,7 @@
     row_base = jnp.arange(request_count, dtype=jnp.int32)[:, None] * node_count
     picked_rows = (row_base + accepted_nodes).reshape(-1)
     picked_hidden = jnp.take(tree_hidden, picked_rows, axis=0)
-    accepted_hidden = lax.all_gather(picked_hidden, "dp", axis=0, tiled=True)
+    accepted_hidden = open_surface_on_mesh(picked_hidden)
     return (tree_hidden, accepted_hidden)
 
 

time: 306 us -> 324 us (1.059)
  waiting for transfers between devices: 126 us -> 174 us
  blocking collectives: 82.7 us -> 51.1 us
    ppermute x0 -> x7, waiting for transfers between devices: none -> 47.8 us  [turn_map_over_axis(): lax.ppermute(all_blocks[-1], device_axis, [(d, (d + 1) % nodes) for d in...]
    all_gather x1 -> x0, blocking collectives: 31.6 us -> none  [per_device(): accepted_hidden = lax.all_gather(picked_hidden, 'dp', axis=0, tiled=True)]
    unnamed x14 -> x27, local copies, waits for them, and re-layouts: 14.7 us -> 14.2 us
  transfers between devices with their start and end apart: 2 -> 9, of which waited for: 2 -> 9; matrix products, arithmetic and copies ran while one was open for 0% -> 0% of each run, Pallas kernels for 0% -> 0%
where the time goes in v1:
time: 324 us; the launch traced here: 323 us
  waiting for transfers between devices  174 us (54%)
  blocking collectives  51.1 us (16%)
  matrix products  45.3 us (14%)
  local copies, waits for them, and re-layouts  20.3 us (6%)
  other arithmetic  16.5 us (5%)
  between operations  14.3 us (4%)
    all_gather x1, waiting for transfers between devices, per_device(): lax.all_gather(attended, 'dp', axis=0, tiled=True)  75.6 us
    all_to_all x1, blocking collectives, per_device(): lax.all_to_all(all_rows.astype(jnp.bfloat16), 'dp', split_axis=0, concat_...  51.1 us
    psum x1, waiting for transfers between devices, per_device(): lax.psum(partial_sum.astype(jnp.bfloat16), 'mp').astype(jnp.float32)  50.2 us
    ppermute x7, waiting for transfers between devices, turn_map_over_axis(): lax.ppermute(all_blocks[-1], device_axis, [(d, (d + 1) % nodes) for d in...  47.8 us
    dot_general x8, matrix products, absorb(): jnp.einsum('rnkgp,rpkd->rnkgd', block_weights.astype(jnp.bfloat16), value...  19.8 us
    dot_general x8, matrix products, absorb(): jnp.einsum('rnkgd,rpkd->rnkgp', query_grid, key_block, preferred_element_...  14.6 us
    unnamed x27, local copies, waits for them, and re-layouts  14.2 us
    reduce_sum x8, other arithmetic, absorb(): new_sum = old_sum * rescale + jnp.sum(block_weights, axis=-1)  13.6 us
  transfers between devices with their start and end apart: 9, of which 9 were waited for; matrix products, arithmetic and copies ran while one was open for 0% of the time, Pallas kernels for 0%

profile of v1, /device:TPU:0, one launch (start us, length us, event | category | flops | bytes accessed | tf_op | source)
XLA Modules:
  0.0 323.2 jit_solution(9475230920322701339)
XLA Ops:
  13.3 6.4 %copy.23 = bf16[2,4096,256]{1,2,0:T(8,128)(2,1)} copy(bf16[2,4096,256]{2,1,0:T(8,128)(2,1)} %param.15) | data formatting | bytes 8388608 | tf_op args[3]
  19.7 6.5 %copy.24 = bf16[2,4096,256]{1,2,0:T(8,128)(2,1)} copy(bf16[2,4096,256]{2,1,0:T(8,128)(2,1)} %param.16) | data formatting | bytes 8388608 | tf_op args[4]
  26.2 49.3 %while.17 = (s32[]{:T(128)}, f32[2,64,2,8]{1,3,2,0:T(8,128)S(1)}, f32[2,64,2,8]{1,3,2,0:T(8,128)S(1)}, f32[2,64,2,8,128]{4,1,3,2,0:T(8,128)S(1)}, s32[2]{0:T(128...) while((s32[]{:T(128)}, f32[2,64,2,8]{1,3,2,0:T(8,128)S(1)}, ...), condition=%wide.region_5.6_spmd, body=%wide.region_2.5_spmd.sunk | while | flops 548935168 | bytes 16392375 | solution.py:112
  26.3 1.8 bitcast_reduce_fusion.2
  28.1 1.7 fusion.61
  29.9 2.5 fusion.62
  32.5 1.8 bitcast_reduce_fusion.2
  36.0 2.5 fusion.62
  38.6 1.8 bitcast_reduce_fusion.2
  40.5 1.7 fusion.61
  42.2 2.5 fusion.62
  44.8 1.8 bitcast_reduce_fusion.2
  48.4 2.5 fusion.62
  51.0 1.8 bitcast_reduce_fusion.2
  54.6 2.5 fusion.62
  57.1 1.8 bitcast_reduce_fusion.2
  60.7 2.5 fusion.62
  63.3 1.8 bitcast_reduce_fusion.2
  66.9 2.5 fusion.62
  69.5 1.8 bitcast_reduce_fusion.2
  73.1 2.5 fusion.62
  77.3 75.6 %all-gather.2.cloned.1.call-done = bf16[1024,2048]{1,0:T(8,128)(2,1)} async-done(((bf16[128,2048]{1,0:T(8,128)(2,1)}), bf16[1024,2048]{1,0:T(8,128)(2,1)}) %all-gather.2.cloned.1.call-update) | async-done | bytes 4194320 | tf_op jit(solution)/shard_map/all_gather | solution.py:117
  153.0 7.9 %convolution_convert_fusion = bf16[1024,1024]{1,0:T(8,128)(2,1)S(1)} fusion(bf16[1024,2048]{1,0:T(8,128)(2,1)} %all-gather.2.cloned.1.call-done, bf16[2048,1024]{1,0:T(8,128)(2,1)} %param.21), kind=kOutput, calls=%fused_computation.27 | convolution fusion | flops 4296015872 | bytes 10485760 | tf_op jit(solution)/shard_map/dot_general | solution.py:116
  160.9 51.1 %all_to_all.19 = bf16[8,128,1024]{2,1,0:T(8,128)(2,1)S(1)} all-to-all(bf16[8,128,1024]{2,1,0:T(8,128)(2,1)S(1)} %bitcast.87), channel_id=1, replica_groups=mesh['dp'=8,'mp'=4] {'dp'}, dimensions={0} | all-to-all | bytes 4194304 | tf_op jit(solution)/shard_map/all_to_all | solution.py:121
  213.9 50.2 %all-reduce.2.cloned.1.call-done = bf16[128,8192]{1,0:T(8,128)(2,1)} async-done(((bf16[128,8192]{1,0:T(8,128)(2,1)}), bf16[128,8192]{1,0:T(8,128)(2,1)}) %all-reduce.2.cloned.1.call-update) | async-done | bytes 2097168 | tf_op jit(solution)/shard_map/psum | solution.py:124
  267.4 5.5 %collective-permute-done = bf16[16,2048]{1,0:T(8,128)(2,1)S(1)} collective-permute-done((bf16[16,2048]{1,0:T(8,128)(2,1)S(1)}, bf16[16,2048]{1,0:T(8,128)(2,1)S(1)}, u32[]{:S(2)}, u32[]{:S(2)}) %collective-permute-start) | collective-permute-done | bytes 65568 | tf_op jit(solution)/shard_map/ppermute | solution.py:19
  272.8 7.0 %collective-permute-done.1 = bf16[16,2048]{1,0:T(8,128)(2,1)S(1)} collective-permute-done((bf16[16,2048]{1,0:T(8,128)(2,1)S(1)}, bf16[16,2048]{1,0:T(8,128)(2,1)S(1)}, u32[]{:S(2)}, u32[]{:S(2)}) %collective-permute-start.1) | collective-permute-done | bytes 65568 | tf_op jit(solution)/shard_map/ppermute | solution.py:19
  279.8 7.0 %collective-permute-done.2 = bf16[16,2048]{1,0:T(8,128)(2,1)S(1)} collective-permute-done((bf16[16,2048]{1,0:T(8,128)(2,1)S(1)}, bf16[16,2048]{1,0:T(8,128)(2,1)S(1)}, u32[]{:S(2)}, u32[]{:S(2)}) %collective-permute-start.2) | collective-permute-done | bytes 65568 | tf_op jit(solution)/shard_map/ppermute | solution.py:19
  286.8 7.0 %collective-permute-done.3 = bf16[16,2048]{1,0:T(8,128)(2,1)S(1)} collective-permute-done((bf16[16,2048]{1,0:T(8,128)(2,1)S(1)}, bf16[16,2048]{1,0:T(8,128)(2,1)S(1)}, u32[]{:S(2)}, u32[]{:S(2)}) %collective-permute-start.3) | collective-permute-done | bytes 65568 | tf_op jit(solution)/shard_map/ppermute | solution.py:19
  293.7 7.5 %collective-permute-done.4 = bf16[16,2048]{1,0:T(8,128)(2,1)S(1)} collective-permute-done((bf16[16,2048]{1,0:T(8,128)(2,1)S(1)}, bf16[16,2048]{1,0:T(8,128)(2,1)S(1)}, u32[]{:S(2)}, u32[]{:S(2)}) %collective-permute-start.4) | collective-permute-done | bytes 65568 | tf_op jit(solution)/shard_map/ppermute | solution.py:19
  301.2 7.0 %collective-permute-done.5 = bf16[16,2048]{1,0:T(8,128)(2,1)S(1)} collective-permute-done((bf16[16,2048]{1,0:T(8,128)(2,1)S(1)}, bf16[16,2048]{1,0:T(8,128)(2,1)S(1)}, u32[]{:S(2)}, u32[]{:S(2)}) %collective-permute-start.5) | collective-permute-done | bytes 65568 | tf_op jit(solution)/shard_map/ppermute | solution.py:19
  308.2 7.0 %collective-permute-done.6 = bf16[16,2048]{1,0:T(8,128)(2,1)S(1)} collective-permute-done((bf16[16,2048]{1,0:T(8,128)(2,1)S(1)}, bf16[16,2048]{1,0:T(8,128)(2,1)S(1)}, u32[]{:S(2)}, u32[]{:S(2)}) %collective-permute-start.6) | collective-permute-done | bytes 65568 | tf_op jit(solution)/shard_map/ppermute | solution.py:19
  (115 shorter events, 25.0 us)
Async XLA Ops:
  7.2 5.6 %copy-start.2 = (bf16[128,256]{1,0:T(8,128)(2,1)S(1)}, bf16[128,256]{1,0:T(8,128)(2,1)}, u32[]{:S(2)}) copy-start(bf16[128,256]{1,0:T(8,128)(2,1)} %param.14) | copy-start | bytes 196612
  7.2 145.8 %all-gather.2.cloned.1.call-start = ((), (), s32[]{:S(2)}) async-start(), calls=%async_computation.1 | async-start | bytes 4718592 | tf_op jit(solution)/shard_map/all_gather | solution.py:117
  19.7 6.5 %copy-start.3 = (s32[2]{0:T(128)S(1)}, s32[2]{0:T(128)}, u32[]{:S(2)}) copy-start(s32[2]{0:T(128)} %param.17) | copy-start | bytes 28
  77.3 186.7 %all-reduce.2.cloned.1.call-start = ((), (), s32[]{:S(2)}) async-start(), calls=%async_computation.2 | async-start | bytes 4194304 | tf_op jit(solution)/shard_map/psum | solution.py:124
  212.1 1.5 copy-start.4
  212.1 52.0 %copy-start.1 = (bf16[128,2048]{1,0:T(8,128)(2,1)S(1)}, bf16[128,2048]{1,0:T(8,128)(2,1)}, u32[]{:S(2)}) copy-start(bf16[128,2048]{1,0:T(8,128)(2,1)} %param.20) | copy-start | bytes 1572868
  265.2 51.2 %copy-start = (bf16[128,2048]{1,0:T(8,128)(2,1)}, bf16[128,2048]{1,0:T(8,128)(2,1)S(1)}, u32[]{:S(2)}) copy-start(bf16[128,2048]{1,0:T(8,128)(2,1)S(1)} %add_convert_fusion) | copy-start | bytes 1572868
  265.9 7.0 %collective-permute-start = (bf16[16,2048]{1,0:T(8,128)(2,1)S(1)}, bf16[16,2048]{1,0:T(8,128)(2,1)S(1)}, u32[]{:S(2)}, u32[]{:S(2)}) collective-permute-start(bf16[16,2048]{1,0:T(8,128)(2,1)S(1)} %broadcast_select_fusion), channel_id=1, source_target_pairs={{0,4},{4,8},{8,12},{12,16},{16,20},{20,24},{24,28},{28,0},{1,5},{5... | collective-permute-start | bytes 196616 | tf_op jit(solution)/shard_map/ppermute | solution.py:19
  272.8 7.0 %collective-permute-start.1 = (bf16[16,2048]{1,0:T(8,128)(2,1)S(1)}, bf16[16,2048]{1,0:T(8,128)(2,1)S(1)}, u32[]{:S(2)}, u32[]{:S(2)}) collective-permute-start(bf16[16,2048]{1,0:T(8,128)(2,1)S(1)} %collective-permute-done), channel_id=1, source_target_pairs={{0,4},{4,8},{8,12},{12,16},{16,20},{20,24},{24,28},{28,0},{1,5},{5... | collective-permute-start | bytes 196616 | tf_op jit(solution)/shard_map/ppermute | solution.py:19
  279.8 7.0 %collective-permute-start.2 = (bf16[16,2048]{1,0:T(8,128)(2,1)S(1)}, bf16[16,2048]{1,0:T(8,128)(2,1)S(1)}, u32[]{:S(2)}, u32[]{:S(2)}) collective-permute-start(bf16[16,2048]{1,0:T(8,128)(2,1)S(1)} %collective-permute-done.1), channel_id=1, source_target_pairs={{0,4},{4,8},{8,12},{12,16},{16,20},{20,24},{24,28},{28,0},{1,5},{5... | collective-permute-start | bytes 196616 | tf_op jit(solution)/shard_map/ppermute | solution.py:19
  286.8 7.0 %collective-permute-start.3 = (bf16[16,2048]{1,0:T(8,128)(2,1)S(1)}, bf16[16,2048]{1,0:T(8,128)(2,1)S(1)}, u32[]{:S(2)}, u32[]{:S(2)}) collective-permute-start(bf16[16,2048]{1,0:T(8,128)(2,1)S(1)} %collective-permute-done.2), channel_id=1, source_target_pairs={{0,4},{4,8},{8,12},{12,16},{16,20},{20,24},{24,28},{28,0},{1,5},{5... | collective-permute-start | bytes 196616 | tf_op jit(solution)/shard_map/ppermute | solution.py:19
  293.7 7.5 %collective-permute-start.4 = (bf16[16,2048]{1,0:T(8,128)(2,1)S(1)}, bf16[16,2048]{1,0:T(8,128)(2,1)S(1)}, u32[]{:S(2)}, u32[]{:S(2)}) collective-permute-start(bf16[16,2048]{1,0:T(8,128)(2,1)S(1)} %collective-permute-done.3), channel_id=1, source_target_pairs={{0,4},{4,8},{8,12},{12,16},{16,20},{20,24},{24,28},{28,0},{1,5},{5... | collective-permute-start | bytes 196616 | tf_op jit(solution)/shard_map/ppermute | solution.py:19
  301.2 7.0 %collective-permute-start.5 = (bf16[16,2048]{1,0:T(8,128)(2,1)S(1)}, bf16[16,2048]{1,0:T(8,128)(2,1)S(1)}, u32[]{:S(2)}, u32[]{:S(2)}) collective-permute-start(bf16[16,2048]{1,0:T(8,128)(2,1)S(1)} %collective-permute-done.4), channel_id=1, source_target_pairs={{0,4},{4,8},{8,12},{12,16},{16,20},{20,24},{24,28},{28,0},{1,5},{5... | collective-permute-start | bytes 196616 | tf_op jit(solution)/shard_map/ppermute | solution.py:19
  308.2 7.0 %collective-permute-start.6 = (bf16[16,2048]{1,0:T(8,128)(2,1)S(1)}, bf16[16,2048]{1,0:T(8,128)(2,1)S(1)}, u32[]{:S(2)}, u32[]{:S(2)}) collective-permute-start(bf16[16,2048]{1,0:T(8,128)(2,1)S(1)} %collective-permute-done.5), channel_id=1, source_target_pairs={{0,4},{4,8},{8,12},{12,16},{16,20},{20,24},{24,28},{28,0},{1,5},{5... | collective-permute-start | bytes 196616 | tf_op jit(solution)/shard_map/ppermute | solution.py:19
Sparse Core Ops, SparseCore 0:
  77.4 75.5 all-gather.1
  213.7 50.2 all-reduce.1
